TPU v7x, 32 devices: a whole 2x2x4 slice. The times are simulated.
32 devices in a mesh: branch: 4 (over x, core), shard: 8 (over z, y).
Axes of the slice: x: 2, y: 2, z: 4, core: 2. Of those that a mesh axis runs over, the one named last changes fastest.
Arguments:
- attention_weights: bfloat16 [4, 2, 4096, 4096], P('branch', None, None, 'shard'), may hold values from -1.25 to 1.25
- ffn_weights: bfloat16 [4, 3, 4096, 11008], P('branch', None, 'shard'), may hold values from -0.3125 to 0.3125
- tokens: bfloat16 [512, 4096], P(('branch', 'shard')), may hold values from -6 to 6
- routes: int32 [512, 2], P(('branch', 'shard')), may hold values from 0 to 3, all different within a row; in each aligned block of 16 rows (0 to 15, 16 to 31, ...) at most 12 rows name the same one
- router: bfloat16 [4096, 4], replicated, may hold values from -0.09375 to 0.09375
Outputs:
- merged_attention: bfloat16 [2, 4096, 4096], P(None, 'branch', 'shard')
- expert_weights: bfloat16 [4, 3, 4096, 11008], P('branch', None, None, 'shard')
- mixed_output: bfloat16 [512, 4096], P(('branch', 'shard'))
Inputs may be any that keep to these rules, and one draw needn't show every extreme that they name: `routes`: the 2 experts of a row differ. In each aligned block of 16 rows (the rows of one device) no expert is named by more than 12 rows, and in some blocks one expert is named by exactly 12 rows.
All inputs are finite; a program needn't handle non-finite values.
Results may differ from a plain program's by a relative error of at most 0.018.
Values may be sent and summed in bfloat16 or wider, within the bound.
No kernel may reach another device: no remote copies, remote signals or barrier semaphores. Data moves between devices by JAX's collectives and lax.ppermute only.
A program may use at most 256 MiB of HBM per device.

v0:
```python
import jax
import jax.numpy as jnp
from jax import lax
from jax.sharding import PartitionSpec as P


def slot_table(route_rows, experts_count, capacity):
    chosen = (route_rows[:, :, None] == jnp.arange(experts_count, dtype=jnp.int32)).astype(
        jnp.int32
    )
    flat_picks = chosen.reshape(-1, experts_count)
    before = jnp.cumsum(flat_picks, axis=0) - flat_picks
    position = jnp.sum(before * flat_picks, axis=1)
    slot_id = route_rows.reshape(-1) * capacity + position
    one_hot = (slot_id[:, None] == jnp.arange(experts_count * capacity, dtype=jnp.int32)).astype(
        jnp.float32
    )
    return jnp.sum(one_hot.reshape(route_rows.shape[0], route_rows.shape[1], -1), axis=1)


def local(attention_weights, ffn_weights, tokens, routes, router):
    branches = lax.axis_size("branch")
    expert_weights = lax.all_to_all(ffn_weights, "shard", split_axis=3, concat_axis=2, tiled=True)
    gate_weight = expert_weights[0, 0]
    up_weight = expert_weights[0, 1]
    down_weight = expert_weights[0, 2]
    tok_count = tokens.shape[0]
    model_width = tokens.shape[1]
    capacity = 3 * tok_count // 4
    slot_map = slot_table(routes, branches, capacity)
    buffers = lax.dot_general(
        slot_map.astype(jnp.bfloat16),
        tokens,
        (((0,), (0,)), ((), ())),
        preferred_element_type=jnp.float32,
    )
    buffers = buffers.astype(jnp.bfloat16).reshape(branches, capacity, model_width)
    arrived = lax.all_to_all(buffers, "branch", split_axis=0, concat_axis=0, tiled=True)
    slot_rows = lax.all_gather(
        arrived.reshape(branches * capacity, model_width), "shard", axis=0, tiled=True
    )
    gate_proj = jnp.dot(slot_rows, gate_weight, preferred_element_type=jnp.float32)
    up_proj = jnp.dot(slot_rows, up_weight, preferred_element_type=jnp.float32)
    hidden = (jax.nn.silu(gate_proj) * up_proj).astype(jnp.bfloat16)
    summed = lax.psum_scatter(
        lax.dot_general(
            hidden, down_weight, (((1,), (1,)), ((), ())), preferred_element_type=jnp.float32
        ).astype(jnp.bfloat16),
        "shard",
        scatter_dimension=0,
        tiled=True,
    )
    outputs = summed.reshape(branches, capacity, model_width)
    returned = lax.all_to_all(outputs, "branch", split_axis=0, concat_axis=0, tiled=True)
    gates_all = jax.nn.sigmoid(jnp.dot(tokens, router, preferred_element_type=jnp.float32))
    weighting = slot_map * jnp.repeat(gates_all, capacity, axis=1)
    mixed_output = jnp.dot(
        weighting,
        returned.reshape(branches * capacity, model_width).astype(jnp.float32),
        precision=lax.Precision.HIGHEST,
    )
    mixed_output = mixed_output.astype(jnp.bfloat16)
    traded = lax.all_to_all(attention_weights, "branch", split_axis=2, concat_axis=0, tiled=True)
    summed_attention = jnp.sum(traded.astype(jnp.float32), axis=0)
    merged_attention = (summed_attention * (1.0 / branches)).astype(jnp.bfloat16)
    return (merged_attention, expert_weights, mixed_output)


def solution(mesh):
    placed = (
        P("branch", None, None, "shard"),
        P("branch", None, "shard", None),
        P(("branch", "shard"), None),
        P(("branch", "shard"), None),
        P(),
    )
    return jax.shard_map(
        local,
        mesh=mesh,
        in_specs=placed,
        out_specs=(
            P(None, "branch", "shard"),
            P("branch", None, None, "shard"),
            P(("branch", "shard"), None),
        ),
        check_vma=False,
    )
```

profile of v0, /device:TPU:0, one launch (start us, length us, event | category | flops | bytes accessed | tf_op | source)
XLA Modules:
  0.0 1343.9 jit_solution(13683050094331782868)
XLA Ops:
  7.2 0.8 copy.62
  8.0 0.1 eq.30
  8.2 0.2 select_reduce_fusion
  8.4 0.1 reduce_sum.33
  8.5 0.1 copy.63
  8.5 0.7 multiply_add_fusion
  9.3 0.3 convolution_convert_fusion
  9.6 0.9 reshape.45
  10.5 4.2 all-to-all-start.2
  14.7 70.5 %copy.59 = bf16[1,3,512,11008]{2,1,0,3:T(4,128)(2,1)} copy(bf16[1,3,512,11008]{3,2,1,0:T(8,128)(2,1)} %param.6) | data formatting | bytes 67633152 | tf_op args[1]
  85.2 8.1 all-to-all-start.1
  93.4 0.8 reshape.46
  94.3 16.4 %copy.58 = bf16[1,2,4096,512]{3,1,0,2:T(2,128)(2,1)} copy(bf16[1,2,4096,512]{3,2,1,0:T(8,128)(2,1)} %param.5) | data formatting | bytes 16777216 | tf_op args[0]
  110.6 991.8 %all-to-all-done.1 = bf16[1,3,512,11008]{2,1,0,3:T(4,128)(2,1)} async-done(((bf16[1,3,512,11008]{2,1,0,3:T(4,128)(2,1)}), bf16[1,3,512,11008]{2,1,0,3:T(4,128)(2,1)}, u32[]{:S(2)}, u32[]{:S(2)}) %all-to-all-start.1) | async-done | bytes 33816608 | tf_op jit(solution)/shard_map/all_to_all | solution.py:23
  1102.4 5.7 all-to-all-start
  1108.1 0.2 reduce-scatter.2.cloned.1.call-start
  1108.3 27.0 %copy.60 = bf16[1,3,512,11008]{2,3,1,0:T(8,128)(2,1)} copy(bf16[1,3,512,11008]{2,1,0,3:T(4,128)(2,1)} %all-to-all-done.1) | data formatting | bytes 67633152 | tf_op jit(solution)/shard_map/all_to_all | solution.py:23
  1135.3 40.4 %copy.61 = bf16[1,3,8,512,1376]{4,3,2,1,0:T(8,128)(2,1)} copy(bf16[1,3,8,512,1376]{3,4,2,1,0:T(8,128)(2,1)} %bitcast.43) | data formatting | bytes 67633152 | tf_op jit(solution)/shard_map/all_to_all | solution.py:23
  1175.8 10.4 fusion.2
  1186.2 19.1 %fusion.3 = bf16[384,4096]{1,0:T(8,128)(2,1)} fusion(bf16[1,3,4096,1376]{3,2,1,0:T(8,128)(2,1)} %bitcast.41, bf16[384,4096]{1,0:T(8,128)(2,1)} %all-gather.2.cloned.1.call-done, f32[384,1376]{0,1:T(8,128)S(1)} %fusion.2), kind=kOutput, calls=%fused_computation.7 | convolution fusion | flops 8661786624 | bytes 31473664 | tf_op jit(solution)/shard_map/dot_general | solution.py:46
  1205.3 0.1 reduce_sum.35
  1205.4 0.2 fusion.9
  1205.6 0.1 copy.64
  1205.7 0.1 broadcast_multiply_fusion
  1205.8 13.3 convert_reduce_fusion
  1219.1 59.9 %reduce-scatter.2.cloned.1.call-done = bf16[48,4096]{1,0:T(8,128)(2,1)} async-done(((bf16[384,4096]{1,0:T(8,128)(2,1)}), bf16[48,4096]{1,0:T(8,128)(2,1)}) %reduce-scatter.2.cloned.1.call-update) | async-done | bytes 393232 | tf_op jit(solution)/shard_map/reduce_scatter | solution.py:45
  1279.0 1.9 reshape.47
  1280.9 3.7 all-to-all-start.3
  1284.6 4.1 multiply_convert_fusion
  1288.7 1.7 copy.66
  1290.4 45.3 %copy.67 = bf16[1,3,4096,1376]{2,3,1,0:T(8,128)(2,1)} copy(bf16[1,3,4096,1376]{3,2,1,0:T(8,128)(2,1)} %bitcast.42) | data formatting | bytes 67633152
  1335.7 1.3 fusion.4
  (14 shorter events, 0.3 us)
Async XLA Ops:
  7.2 2.2 copy-start
  10.5 74.7 %all-to-all-start.2 = ((bf16[4,12,4096]{2,1,0:T(8,128)(2,1)}), bf16[4,12,4096]{2,1,0:T(8,128)(2,1)S(1)}, u32[]{:S(2)}, u32[]{:S(2)}) async-start(bf16[4,12,4096]{2,1,0:T(8,128)(2,1)} %reshape.45), calls=%async_computation.2 | async-start | bytes 1048576 | tf_op jit(solution)/shard_map/all_to_all | solution.py:38
  85.2 1017.2 %all-to-all-start.1 = ((bf16[1,3,512,11008]{2,1,0,3:T(4,128)(2,1)}), bf16[1,3,512,11008]{2,1,0,3:T(4,128)(2,1)}, u32[]{:S(2)}, u32[]{:S(2)}) async-start(bf16[1,3,512,11008]{2,1,0,3:T(4,128)(2,1)} %copy.59), calls=%async_computation.1 | async-start | bytes 90177536 | tf_op jit(solution)/shard_map/all_to_all | solution.py:23
  93.4 1082.4 %all-gather.2.cloned.1.call-start = ((), (), s32[]{:S(2)}) async-start(), calls=%async_computation.5 | async-start | bytes 3538944 | tf_op jit(solution)/shard_map/all_gather | solution.py:39
  1102.4 103.4 %all-to-all-start = ((bf16[1,2,4096,512]{3,1,0,2:T(2,128)(2,1)}), bf16[1,2,4096,512]{3,1,0,2:T(2,128)(2,1)}, u32[]{:S(2)}, u32[]{:S(2)}) async-start(bf16[1,2,4096,512]{3,1,0,2:T(2,128)(2,1)} %copy.58), calls=%async_computation | async-start | bytes 16777216 | tf_op jit(solution)/shard_map/all_to_all | solution.py:63
  1108.1 171.0 %reduce-scatter.2.cloned.1.call-start = ((), (), s32[]{:S(2)}) async-start(), calls=%async_computation.6 | async-start | bytes 3538944 | tf_op jit(solution)/shard_map/reduce_scatter | solution.py:45
  1186.2 19.3 %copy-start.1 = (bf16[4096,4]{0,1:T(4,128)(2,1)S(1)}, bf16[4096,4]{0,1:T(4,128)(2,1)}, u32[]{:S(2)}) copy-start(bf16[4096,4]{0,1:T(4,128)(2,1)} %param.9) | copy-start | bytes 98308
  1280.9 54.8 %all-to-all-start.3 = ((bf16[4,12,4096]{2,1,0:T(8,128)(2,1)}), bf16[4,12,4096]{2,1,0:T(8,128)(2,1)S(1)}, u32[]{:S(2)}, u32[]{:S(2)}) async-start(bf16[4,12,4096]{2,1,0:T(8,128)(2,1)} %reshape.47), calls=%async_computation.4 | async-start | bytes 1048576 | tf_op jit(solution)/shard_map/all_to_all | solution.py:54
Sparse Core Ops, SparseCore 0:
  96.9 777.9 all-gather.1
  1205.5 73.5 reduce-scatter.1
where the time goes:
time: 1350 us; the launch traced here: 1340 us
  waiting for transfers between devices  1050 us (78%)
  local copies, waits for them, and re-layouts  206 us (15%)
  matrix products  31.3 us (2%)
  starting transfers between devices  22 us (2%)
  other arithmetic  18.6 us (1%)
  between operations  14.1 us (1%)
    all_to_all x1, waiting for transfers between devices, local(): lax.all_to_all(ffn_weights, 'shard', split_axis=3, concat_axis=2, tiled=T...  992 us
    unnamed x9, local copies, waits for them, and re-layouts  135 us
    all_to_all x2, local copies, waits for them, and re-layouts, local(): lax.all_to_all(ffn_weights, 'shard', split_axis=3, concat_axis=2, tiled=T...  67.5 us
    reduce_scatter x1, waiting for transfers between devices, local(): lax.psum_scatter(lax.dot_general(hidden, down_weight, (((1,), (1,)), ((),...  59.9 us
  transfers between devices with their start and end apart: 6, of which 2 were waited for; matrix products, arithmetic and copies ran while one was open for 19% of the time, Pallas kernels for 0%

commit v1 on v0

--- a/solution.py
+++ b/solution.py
@@ -1,6 +1,8 @@
 import jax
 import jax.numpy as jnp
 from jax import lax
+from jax.experimental import pallas as pl
+from jax.experimental.pallas import tpu as pltpu
 from jax.sharding import PartitionSpec as P
 
 
@@ -18,12 +20,132 @@
     return jnp.sum(one_hot.reshape(route_rows.shape[0], route_rows.shape[1], -1), axis=1)
 
 
+def turn_body(source, target):
+    target[...] = source[0, 0].T
+
+
+def turned(ffn_weights, which):
+    rows, hidden_units = ffn_weights.shape[2:]
+    lanes = next(
+        128 * n for n in range(16, 0, -1) if hidden_units % (128 * n) == 0 and n * rows <= 4096
+    )
+    return pl.pallas_call(
+        turn_body,
+        grid=(hidden_units // lanes,),
+        in_specs=[pl.BlockSpec((1, 1, rows, lanes), lambda i: (0, which, 0, i))],
+        out_specs=pl.BlockSpec((lanes, rows), lambda i: (i, 0)),
+        out_shape=jax.ShapeDtypeStruct((hidden_units, rows), ffn_weights.dtype),
+        name=f"turn_{which}",
+    )(ffn_weights)
+
+
+CONTRACT_LAST = (((1,), (1,)), ((), ()))
+
+
+def gate_body(rows, piece, placed, product):
+    step = pl.program_id(0)
+    weight = piece[0]
+    placed[0] = weight
+    part = lax.dot_general(rows[...], weight, CONTRACT_LAST, preferred_element_type=jnp.float32)
+
+    @pl.when(step == 0)
+    def _():
+        product[...] = part
+
+    @pl.when(step > 0)
+    def _():
+        product[...] += part
+
+
+def up_body(rows, piece, gate, whole, placed, hidden, total):
+    del whole
+    step = pl.program_id(0)
+    weight = piece[0]
+    placed[0] = weight
+    part = lax.dot_general(rows[...], weight, CONTRACT_LAST, preferred_element_type=jnp.float32)
+
+    @pl.when(step == 0)
+    def _():
+        total[...] = part
+
+    @pl.when(step > 0)
+    def _():
+        total[...] += part
+
+    @pl.when(step == pl.num_programs(0) - 1)
+    def _():
+        value = gate[...]
+        hidden[...] = (value / (1.0 + jnp.exp(-value)) * total[...]).astype(hidden.dtype)
+
+
+def down_body(hidden, piece, whole, placed, product):
+    del whole
+    weight = piece[0]
+    placed[0] = weight
+    product[...] = jnp.dot(hidden[...], weight, preferred_element_type=jnp.float32).astype(
+        product.dtype
+    )
+
+
+def expert_kernels(pieces_of, slot_rows, merged_attention):
+    slots, model_width = slot_rows.shape
+
+    def specs(which, pieces):
+        count, units, rows = pieces.shape
+        return (
+            pl.BlockSpec((1, units, rows), lambda j: (j, 0, 0)),
+            pl.BlockSpec((1, units, rows), lambda j: (which, 0, j)),
+            pl.BlockSpec((slots, rows), lambda j: (0, j)),
+            pl.BlockSpec((slots, units), lambda j: (0, 0)),
+            jax.ShapeDtypeStruct((3, units, model_width), pieces.dtype),
+            jax.ShapeDtypeStruct((slots, units), jnp.float32),
+        )
+
+    def gate_step(pieces):
+        piece, placed, row_block, full, whole_shape, product_shape = specs(0, pieces)
+        return pl.pallas_call(
+            gate_body,
+            grid=(pieces.shape[0],),
+            in_specs=[row_block, piece],
+            out_specs=[placed, full],
+            out_shape=[whole_shape, product_shape],
+            name="gate_step",
+        )(slot_rows, pieces)
+
+    def up_step(pieces, gate, whole):
+        piece, placed, row_block, full, whole_shape, product_shape = specs(1, pieces)
+        return pl.pallas_call(
+            up_body,
+            grid=(pieces.shape[0],),
+            in_specs=[row_block, piece, full, pl.BlockSpec(memory_space=pl.ANY)],
+            out_specs=[placed, full],
+            out_shape=[whole_shape, jax.ShapeDtypeStruct(product_shape.shape, slot_rows.dtype)],
+            scratch_shapes=[pltpu.VMEM(product_shape.shape, jnp.float32)],
+            input_output_aliases={3: 0},
+            name="up_step",
+        )(slot_rows, pieces, gate, whole)
+
+    def down_step(pieces, hidden, whole):
+        piece, placed, row_block, full, whole_shape, product_shape = specs(2, pieces)
+        return pl.pallas_call(
+            down_body,
+            grid=(pieces.shape[0],),
+            in_specs=[full, piece, pl.BlockSpec(memory_space=pl.ANY)],
+            out_specs=[placed, row_block],
+            out_shape=[whole_shape, jax.ShapeDtypeStruct((slots, model_width), slot_rows.dtype)],
+            input_output_aliases={2: 0},
+            name="down_step",
+        )(hidden, pieces, whole)
+
+    whole, gate = gate_step(pieces_of[0])
+    gate, merged_attention = lax.optimization_barrier((gate, merged_attention))
+    whole, hidden = up_step(pieces_of[1], gate, whole)
+    return (*down_step(pieces_of[2], hidden, whole), merged_attention)
+
+
 def local(attention_weights, ffn_weights, tokens, routes, router):
     branches = lax.axis_size("branch")
-    expert_weights = lax.all_to_all(ffn_weights, "shard", split_axis=3, concat_axis=2, tiled=True)
-    gate_weight = expert_weights[0, 0]
-    up_weight = expert_weights[0, 1]
-    down_weight = expert_weights[0, 2]
+    shards = lax.axis_size("shard")
     tok_count = tokens.shape[0]
     model_width = tokens.shape[1]
     capacity = 3 * tok_count // 4
@@ -39,17 +161,37 @@
     slot_rows = lax.all_gather(
         arrived.reshape(branches * capacity, model_width), "shard", axis=0, tiled=True
     )
-    gate_proj = jnp.dot(slot_rows, gate_weight, preferred_element_type=jnp.float32)
-    up_proj = jnp.dot(slot_rows, up_weight, preferred_element_type=jnp.float32)
-    hidden = (jax.nn.silu(gate_proj) * up_proj).astype(jnp.bfloat16)
-    summed = lax.psum_scatter(
-        lax.dot_general(
-            hidden, down_weight, (((1,), (1,)), ((), ())), preferred_element_type=jnp.float32
-        ).astype(jnp.bfloat16),
-        "shard",
-        scatter_dimension=0,
-        tiled=True,
-    )
+
+    rows = ffn_weights.shape[2]
+    units = ffn_weights.shape[3] // shards
+    pieces_of = [
+        lax.all_to_all(
+            turned(ffn_weights, which).reshape(shards, units, rows),
+            "shard",
+            split_axis=0,
+            concat_axis=0,
+            tiled=True,
+        )
+        for which in range(3)
+    ]
+    mine = lax.axis_index("branch")
+    height = attention_weights.shape[2] // branches
+
+    def block_for(owner):
+        return lax.dynamic_slice_in_dim(attention_weights[0], owner * height, height, 1)
+
+    summed_attention = block_for(mine).astype(jnp.float32)
+    for shift in range(1, branches):
+        moved = lax.ppermute(
+            block_for((mine + shift) % branches),
+            "branch",
+            [(b, (b + shift) % branches) for b in range(branches)],
+        )
+        summed_attention = summed_attention + moved.astype(jnp.float32)
+    merged_attention = (summed_attention * (1.0 / branches)).astype(jnp.bfloat16)
+    whole, partial_value, merged_attention = expert_kernels(pieces_of, slot_rows, merged_attention)
+    expert_weights = jnp.swapaxes(whole, 1, 2)[None]
+    summed = lax.psum_scatter(partial_value, "shard", scatter_dimension=0, tiled=True)
     outputs = summed.reshape(branches, capacity, model_width)
     returned = lax.all_to_all(outputs, "branch", split_axis=0, concat_axis=0, tiled=True)
     gates_all = jax.nn.sigmoid(jnp.dot(tokens, router, preferred_element_type=jnp.float32))
@@ -60,9 +202,6 @@
         precision=lax.Precision.HIGHEST,
     )
     mixed_output = mixed_output.astype(jnp.bfloat16)
-    traded = lax.all_to_all(attention_weights, "branch", split_axis=2, concat_axis=0, tiled=True)
-    summed_attention = jnp.sum(traded.astype(jnp.float32), axis=0)
-    merged_attention = (summed_attention * (1.0 / branches)).astype(jnp.bfloat16)
     return (merged_attention, expert_weights, mixed_output)
 
 

time: 1350 us -> 943 us (0.70)
  waiting for transfers between devices: 1050 us -> 755 us
  local copies, waits for them, and re-layouts: 206 us -> 10.4 us
  Pallas kernels: 0 us -> 124 us
  matrix products: 31.3 us -> 1.78 us
    all_to_all x2 -> x3, waiting for transfers between devices: 992 us -> 452 us  [local(): lax.all_to_all(turned(ffn_weights, which).reshape(shards, units, rows), '...]
    unnamed x9 -> x5, local copies, waits for them, and re-layouts: 135 us -> 0.81 us
    all_gather x1, waiting for transfers between devices: 0.01 us -> 130 us  [local(): lax.all_gather(arrived.reshape(branches * capacity, model_width), 'shard'...]
    pallas_call x0 -> x6, Pallas kernels: none -> 124 us  [the longest x3 81 us: turned(): pl.pallas_call(turn_body, grid=(hidden_units // lanes,), in_specs=[pl.Blo...]
    ppermute x0 -> x3, waiting for transfers between devices: none -> 91.5 us  [local(): lax.ppermute(block_for((mine + shift) % branches), 'branch', [(b, (b + sh...]
    all_to_all x2 -> x0, local copies, waits for them, and re-layouts: 67.5 us -> none  [local(): lax.all_to_all(ffn_weights, 'shard', split_axis=3, concat_axis=2, tiled=T...]
    dot_general x2 -> x0, matrix products: 29.5 us -> none  [the longest x1 19.1 us: local(): lax.dot_general(hidden, down_weight, (((1,), (1,)), ((), ())), preferred_...]
  transfers between devices with their start and end apart: 6 -> 10, of which waited for: 2 -> 9; matrix products, arithmetic and copies ran while one was open for 19% -> 1% of each run, Pallas kernels for 0% -> 12%
where the time goes in v1:
time: 943 us; the launch traced here: 940 us
  waiting for transfers between devices  755 us (80%)
  Pallas kernels  124 us (13%)
  starting transfers between devices  26.4 us (3%)
  between operations  14.2 us (2%)
  local copies, waits for them, and re-layouts  10.4 us (1%)
    all_to_all x3, waiting for transfers between devices, local(): lax.all_to_all(turned(ffn_weights, which).reshape(shards, units, rows), '...  452 us
    all_gather x1, waiting for transfers between devices, local(): lax.all_gather(arrived.reshape(branches * capacity, model_width), 'shard'...  130 us
    ppermute x3, waiting for transfers between devices, local(): lax.ppermute(block_for((mine + shift) % branches), 'branch', [(b, (b + sh...  91.5 us
    pallas_call x3, Pallas kernels, turned(): pl.pallas_call(turn_body, grid=(hidden_units // lanes,), in_specs=[pl.Blo...  81 us
    reduce_scatter x1, waiting for transfers between devices, local(): lax.psum_scatter(partial_value, 'shard', scatter_dimension=0, tiled=True)  73.3 us
  transfers between devices with their start and end apart: 10, of which 9 were waited for; matrix products, arithmetic and copies ran while one was open for 1% of the time, Pallas kernels for 12%

profile of v1, /device:TPU:0, one launch (start us, length us, event | category | flops | bytes accessed | tf_op | source)
XLA Modules:
  0.0 939.5 jit_solution(14677448859214093626)
XLA Ops:
  7.2 0.8 copy.23
  8.2 0.2 select_reduce_fusion
  8.5 0.7 multiply_add_fusion
  9.3 0.3 convolution_convert_fusion
  9.6 0.9 reshape.56
  10.5 4.2 all-to-all-start
  14.7 27.0 %turn_0.1 = bf16[11008,512]{1,0:T(8,128)(2,1)} custom-call(bf16[1,3,512,11008]{3,2,1,0:T(8,128)(2,1)} %source.5), custom_call_target="tpu_custom_call" | custom-call | tf_op jit(solution)/shard_map/turn_0/pallas_call | solution.py:32
  41.8 6.6 all-to-all-start.1
  48.3 26.9 %turn_1.1 = bf16[11008,512]{1,0:T(8,128)(2,1)} custom-call(bf16[1,3,512,11008]{3,2,1,0:T(8,128)(2,1)} %source.5), custom_call_target="tpu_custom_call" | custom-call | tf_op jit(solution)/shard_map/turn_1/pallas_call | solution.py:32
  75.3 218.7 %all-to-all-done.1.piece = bf16[8,1376,512]{2,1,0:T(8,128)(2,1)} async-done(((bf16[8,1376,512]{2,1,0:T(8,128)(2,1)}), bf16[8,1376,512]{2,1,0:T(8,128)(2,1)}, u32[]{:S(2)}, u32[]{:S(2)}) %all-to-all-start.1) | async-done | bytes 11272224 | tf_op jit(solution)/shard_map/all_to_all | solution.py:168
  293.9 5.2 all-to-all-start.2
  299.1 27.0 %turn_2.1 = bf16[11008,512]{1,0:T(8,128)(2,1)} custom-call(bf16[1,3,512,11008]{3,2,1,0:T(8,128)(2,1)} %source.5), custom_call_target="tpu_custom_call" | custom-call | tf_op jit(solution)/shard_map/turn_2/pallas_call | solution.py:32
  326.2 217.6 %all-to-all-done.2.piece = bf16[8,1376,512]{2,1,0:T(8,128)(2,1)} async-done(((bf16[8,1376,512]{2,1,0:T(8,128)(2,1)}), bf16[8,1376,512]{2,1,0:T(8,128)(2,1)}, u32[]{:S(2)}, u32[]{:S(2)}) %all-to-all-start.2) | async-done | bytes 11272224 | tf_op jit(solution)/shard_map/all_to_all | solution.py:168
  543.8 5.2 all-to-all-start.3
  549.1 0.8 reshape.57
  550.0 5.5 dynamic-slice_bitcast_fusion.2
  555.6 1.3 collective-permute-start.1
  556.9 0.2 collective-permute-start
  557.1 43.9 %collective-permute-done.2 = bf16[2,1024,512]{2,1,0:T(8,128)(2,1)} collective-permute-done((bf16[2,1024,512]{2,1,0:T(8,128)(2,1)}, bf16[2,1024,512]{2,1,0:T(8,128)(2,1)}, u32[]{:S(2)}, u32[]{:S(2)}) %collective-permute-start.2) | collective-permute-done | bytes 2097184 | tf_op jit(solution)/shard_map/ppermute | solution.py:185
  601.0 47.4 %collective-permute-done.1 = bf16[2,1024,512]{2,1,0:T(8,128)(2,1)} collective-permute-done((bf16[2,1024,512]{2,1,0:T(8,128)(2,1)}, bf16[2,1024,512]{2,1,0:T(8,128)(2,1)}, u32[]{:S(2)}, u32[]{:S(2)}) %collective-permute-start.1) | collective-permute-done | bytes 2097184 | tf_op jit(solution)/shard_map/ppermute | solution.py:185
  648.4 0.2 collective-permute-done
  648.6 6.0 fusion.4
  654.6 130.0 %all-gather.2.cloned.1.call-done.rows = bf16[384,4096]{1,0:T(8,128)(2,1)} async-done(((bf16[48,4096]{1,0:T(8,128)(2,1)}), bf16[384,4096]{1,0:T(8,128)(2,1)}) %all-gather.2.cloned.1.call-update) | async-done | bytes 3145744 | tf_op jit(solution)/shard_map/all_gather | solution.py:161
  784.6 14.7 %gate_step.1 = (bf16[3,1376,4096]{2,1,0:T(8,128)(2,1)}, f32[384,1376]{1,0:T(8,128)}) custom-call(bf16[384,4096]{1,0:T(8,128)(2,1)} %all-gather.2.cloned.1.call-done.rows, bf16[8,1376,512]{2,1,0:T(8,128)(2,1)} %all-to-all-done.1.piece), custom_call_target="tpu_custom_call" | custom-call | tf_op jit(solution)/shard_map/gate_step/pallas_call | solution.py:106
  799.3 15.6 %up_step.1 = (bf16[3,1376,4096]{2,1,0:T(8,128)(2,1)}, bf16[384,1376]{1,0:T(8,128)(2,1)}) custom-call(bf16[384,4096]{1,0:T(8,128)(2,1)} %all-gather.2.cloned.1.call-done.rows, bf16[8,1376,512]{2,1,0:T(8,128)(2,1)} %all-to-all-done.2.piece, f32[384,1376]{1,0:T(8,128)} %get-tuple-element.13.gate, ...), custom_call_target="tpu_custom_call", output_to_operand_aliasing={{0}: (3, {})} | custom-call | tf_op jit(solution)/shard_map/up_step/pallas_call | solution.py:117
  814.9 15.8 %all-to-all-done.3.piece = bf16[8,1376,512]{2,1,0:T(8,128)(2,1)} async-done(((bf16[8,1376,512]{2,1,0:T(8,128)(2,1)}), bf16[8,1376,512]{2,1,0:T(8,128)(2,1)}, u32[]{:S(2)}, u32[]{:S(2)}) %all-to-all-start.3) | async-done | bytes 11272224 | tf_op jit(solution)/shard_map/all_to_all | solution.py:168
  830.7 13.1 %down_step.1 = (bf16[3,1376,4096]{2,1,0:T(8,128)(2,1)}, bf16[384,4096]{1,0:T(8,128)(2,1)}) custom-call(bf16[384,1376]{1,0:T(8,128)(2,1)} %get-tuple-element.15.hidden, bf16[8,1376,512]{2,1,0:T(8,128)(2,1)} %all-to-all-done.3.piece, bf16[3,1376,4096]{2,1,0:T(8,128)(2,1)} %get-tuple-element.16.whole), custom_call_target="tpu_custom_call", output_to_operand_aliasing={{0}: (2, {})} | custom-call | tf_op jit(solution)/shard_map/down_step/pallas_call | solution.py:130
  843.9 73.3 %reduce-scatter.2.cloned.1.call-done = bf16[48,4096]{1,0:T(8,128)(2,1)} async-done(((bf16[384,4096]{1,0:T(8,128)(2,1)}), bf16[48,4096]{1,0:T(8,128)(2,1)}) %reduce-scatter.2.cloned.1.call-update) | async-done | bytes 393232 | tf_op jit(solution)/shard_map/reduce_scatter | solution.py:194
  917.2 1.9 reshape.61
  919.1 3.5 all-to-all-start.4
  923.0 8.3 all-to-all-done.4
  931.4 1.3 fusion
  (20 shorter events, 1.0 us)
Async XLA Ops:
  7.2 2.2 copy-start
  10.5 31.3 %all-to-all-start = ((bf16[4,12,4096]{2,1,0:T(8,128)(2,1)}), bf16[4,12,4096]{2,1,0:T(8,128)(2,1)S(1)}, u32[]{:S(2)}, u32[]{:S(2)}) async-start(bf16[4,12,4096]{2,1,0:T(8,128)(2,1)} %reshape.56), calls=%async_computation | async-start | bytes 1048576 | tf_op jit(solution)/shard_map/all_to_all | solution.py:160
  41.8 252.2 %all-to-all-start.1 = ((bf16[8,1376,512]{2,1,0:T(8,128)(2,1)}), bf16[8,1376,512]{2,1,0:T(8,128)(2,1)}, u32[]{:S(2)}, u32[]{:S(2)}) async-start(bf16[8,1376,512]{2,1,0:T(8,128)(2,1)} %bitcast.25), calls=%async_computation.1 | async-start | bytes 22544384 | tf_op jit(solution)/shard_map/all_to_all | solution.py:168
  293.9 249.8 %all-to-all-start.2 = ((bf16[8,1376,512]{2,1,0:T(8,128)(2,1)}), bf16[8,1376,512]{2,1,0:T(8,128)(2,1)}, u32[]{:S(2)}, u32[]{:S(2)}) async-start(bf16[8,1376,512]{2,1,0:T(8,128)(2,1)} %bitcast.26), calls=%async_computation.2 | async-start | bytes 22544384 | tf_op jit(solution)/shard_map/all_to_all | solution.py:168
  543.8 287.0 %all-to-all-start.3 = ((bf16[8,1376,512]{2,1,0:T(8,128)(2,1)}), bf16[8,1376,512]{2,1,0:T(8,128)(2,1)}, u32[]{:S(2)}, u32[]{:S(2)}) async-start(bf16[8,1376,512]{2,1,0:T(8,128)(2,1)} %bitcast.24), calls=%async_computation.3 | async-start | bytes 22544384 | tf_op jit(solution)/shard_map/all_to_all | solution.py:168
  549.0 235.6 %all-gather.2.cloned.1.call-start = ((), (), s32[]{:S(2)}) async-start(), calls=%async_computation.6 | async-start | bytes 3538944 | tf_op jit(solution)/shard_map/all_gather | solution.py:161
  549.9 367.3 %reduce-scatter.2.cloned.1.call-start = ((), (), s32[]{:S(2)}) async-start(), calls=%async_computation.7 | async-start | bytes 3538944 | tf_op jit(solution)/shard_map/reduce_scatter | solution.py:194
  555.6 45.5 %collective-permute-start.2 = (bf16[2,1024,512]{2,1,0:T(8,128)(2,1)}, bf16[2,1024,512]{2,1,0:T(8,128)(2,1)}, u32[]{:S(2)}, u32[]{:S(2)}) collective-permute-start(bf16[2,1024,512]{2,1,0:T(8,128)(2,1)} %get-tuple-element.20), channel_id=1, source_target_pairs={{0,24},{8,0},{16,8},{24,16},{1,25},{9,1},{17,9},{25,17},{2,26},{10... | collective-permute-start | bytes 6291464 | tf_op jit(solution)/shard_map/ppermute | solution.py:185
  555.6 92.9 %collective-permute-start.1 = (bf16[2,1024,512]{2,1,0:T(8,128)(2,1)}, bf16[2,1024,512]{2,1,0:T(8,128)(2,1)}, u32[]{:S(2)}, u32[]{:S(2)}) collective-permute-start(bf16[2,1024,512]{2,1,0:T(8,128)(2,1)} %get-tuple-element.21), channel_id=1, source_target_pairs={{0,16},{8,24},{16,0},{24,8},{1,17},{9,25},{17,1},{25,9},{2,18},{10... | collective-permute-start | bytes 6291464 | tf_op jit(solution)/shard_map/ppermute | solution.py:185
  556.9 91.7 %collective-permute-start = (bf16[2,1024,512]{2,1,0:T(8,128)(2,1)S(1)}, bf16[2,1024,512]{2,1,0:T(8,128)(2,1)}, u32[]{:S(2)}, u32[]{:S(2)}) collective-permute-start(bf16[2,1024,512]{2,1,0:T(8,128)(2,1)S(1)} %get-tuple-element.19), channel_id=1, source_target_pairs={{0,8},{8,16},{16,24},{24,0},{1,9},{9,17},{17,25},{25,1},{2,10},{10... | collective-permute-start | bytes 6291464 | tf_op jit(solution)/shard_map/ppermute | solution.py:185
  843.8 78.7 %copy-start.1 = (bf16[4096,4]{0,1:T(4,128)(2,1)S(1)}, bf16[4096,4]{0,1:T(4,128)(2,1)}, u32[]{:S(2)}) copy-start(bf16[4096,4]{0,1:T(4,128)(2,1)} %param.9) | copy-start | bytes 98308
  919.1 12.3 %all-to-all-start.4 = ((bf16[4,12,4096]{2,1,0:T(8,128)(2,1)}), bf16[4,12,4096]{2,1,0:T(8,128)(2,1)S(1)}, u32[]{:S(2)}, u32[]{:S(2)}) async-start(bf16[4,12,4096]{2,1,0:T(8,128)(2,1)} %reshape.61), calls=%async_computation.5 | async-start | bytes 1048576 | tf_op jit(solution)/shard_map/all_to_all | solution.py:196
Sparse Core Ops, SparseCore 0:
  552.0 232.5 all-gather.1
  844.0 73.1 reduce-scatter.1
